TPU v7x, 128 devices: a whole 4x4x4 slice. The times are simulated.
128 devices in a mesh: seq: 8 (over y, core), chan: 16 (over z, x).
Axes of the slice: x: 4, y: 4, z: 4, core: 2. Of those that a mesh axis runs over, the one named last changes fastest.
Arguments:
- scan_input: bfloat16 [2048, 5120], P('seq', 'chan'), may hold values from -6 to 6
- gate_input: bfloat16 [2048, 5120], P('seq', 'chan'), may hold values from -6 to 6
- step_raw: bfloat16 [2048, 5120], P('seq', 'chan')
- log_rates: float32 [16, 5120], P(None, 'chan')
- skip_gain: float32 [5120], P('chan'), may hold values from 0.5 to 1.5
- state_write: float32 [16, 2048], P(None, 'seq'), may hold values from -6 to 6
- state_read: float32 [16, 2048], P(None, 'seq'), may hold values from -6 to 6
- out_weight: bfloat16 [5120, 2560], P('chan'), may hold values from -0.078125 to 0.078125
- out_cotangent: bfloat16 [2048, 2560], P('seq', 'chan'), may hold values from -6 to 6
Outputs:
- grad_input: bfloat16 [2048, 5120], P('seq', 'chan')
- grad_gate: bfloat16 [2048, 5120], P('seq', 'chan')
- grad_step: bfloat16 [2048, 5120], P('seq', 'chan')
- grad_rates: float32 [16, 5120], P(None, 'chan')
- grad_skip: float32 [5120], P('chan')
- grad_write: float32 [16, 2048], P(None, ('seq', 'chan'))
- grad_read: float32 [16, 2048], P(None, ('seq', 'chan'))
- grad_weight: float32 [5120, 2560], P('chan', 'seq')
All inputs are finite; a program needn't handle non-finite values.
Results may differ from a plain program's by a relative error of at most 0.0095.
Values may be sent and summed in bfloat16 or wider, within the bound.
A program may use at most 64 MiB of HBM per device.

v0:
```python
import functools
import math

import jax
import jax.numpy as jnp
from jax import lax
from jax.experimental import pallas as pl
from jax.experimental.pallas import tpu as pltpu
from jax.sharding import PartitionSpec as P

F32, BF16 = jnp.float32, jnp.bfloat16
LOG2E, LN2 = 1.0 / math.log(2.0), math.log(2.0)
T, E, PAD, NS, DM = 256, 320, 384, 16, 2560
SUB, STEPS = 8, 32
FEAT = 160
UNROLL = 2


def sigmoid(v):
    return 1.0 / (1.0 + jnp.exp(-v))


def kernel(
    x_ref, z_ref, st_ref, lr_ref, sk_ref, b_ref, c_ref, w_hbm, do_ref,
    gi_ref, gg_ref, gs_ref, gr_ref, gk_ref, gwrite_ref, gread_ref, gw_ref,
    W, G, GP, DOP, XP, ZP, TP, SKP, LRP, A2N, A2B, BP, BTN, BTP, BB, D, DX, DY, Y, LB, GD,
    DEC, HS, HPRE, HIN, PW, CS, YN, GF, GT, GTP, DGT, DG, PB, SB, RB, XF, XB, XR, R2, GX,
    w_sem, g_send, g_recv, p_send, p_recv, f_send, f_recv, b_send, b_recv, r_send, r_recv,
    n_send, n_recv, x_send, x_recv,
):
    s, c = lax.axis_index("seq"), lax.axis_index("chan")
    kap, chip = s % 2, s // 2
    partner = s + 1 - 2 * kap
    up, down = ((chip + 1) % 4) * 2 + kap, ((chip + 3) % 4) * 2 + kap

    def rc(src, dst, ss, rs, ps, pc):
        return pltpu.make_async_remote_copy(
            src_ref=src, dst_ref=dst, send_sem=ss, recv_sem=rs,
            device_id=(ps, pc), device_id_type=pl.DeviceIdType.MESH,
        )

    w_copy = pltpu.make_async_copy(w_hbm, W, w_sem)
    w_copy.start()
    barrier = pltpu.get_barrier_semaphore()
    for o in range(1, 16):
        pl.semaphore_signal(barrier, inc=1, device_id=(s, (c + o) % 16), device_id_type=pl.DeviceIdType.MESH)
    for o in range(1, 8):
        pl.semaphore_signal(barrier, inc=1, device_id=((s + o) % 8, c), device_id_type=pl.DeviceIdType.MESH)

    DOP[:, FEAT:] = jnp.zeros((T, 256 - FEAT), BF16)
    DOP[:, :FEAT] = do_ref[...]
    own = pl.multiple_of(c * FEAT, 32)
    for tb in range(2):
        rows = slice(128 * tb, 128 * tb + 128)
        first = DOP[rows, :128].astype(F32).T.astype(BF16)
        second = DOP[rows, 128:].astype(F32).T.astype(BF16)
        G[pl.ds(own, 128), rows] = first
        G[pl.ds(own + 128, FEAT - 128), rows] = second[: FEAT - 128]
    pl.semaphore_wait(barrier, 22)

    def g_copy(o):
        q = pl.ds(own, FEAT)
        return rc(G.at[q], G.at[q], g_send.at[o], g_recv.at[o], s, (c + o) % 16)

    gathers = [g_copy(o) for o in range(1, 16)]
    for copy in gathers:
        copy.start()

    for src, dst in ((x_ref, XP), (z_ref, ZP), (st_ref, TP)):
        dst[:, 256:] = jnp.zeros((T, 128), BF16)
        dst[:, :E] = src[...]
    SKP[:, 256:] = jnp.zeros((8, 128), F32)
    SKP[0:1, :E] = sk_ref[...]
    LRP[:, 256:] = jnp.zeros((NS, 128), F32)
    LRP[:, :E] = lr_ref[...]
    for j in range(3):
        A2N[j] = -LOG2E * jnp.exp(LRP[:, 128 * j : 128 * j + 128])
    for n in range(NS):
        for j in range(3):
            tt = (n % 4) * 3 + j
            A2B[n // 4, 8 * tt : 8 * tt + 8, :] = jnp.broadcast_to(A2N[j, n : n + 1, :], (8, 128))

    def lanes(j):
        return slice(128 * j, 128 * j + 128)

    def perm(m, half, j):
        return pl.ds(j * T + 8 * (16 * (m % 2) + 8 * half) + m // 2, 8, stride=8)

    def prologue(m, carry):
        rows = pl.ds(pl.multiple_of(16 * m, 16), 16)
        for j in range(3):
            st = TP[rows, lanes(j)].astype(F32)
            delta = jnp.maximum(st, 0.0) + jnp.log1p(jnp.exp(-jnp.abs(st)))
            dx = delta * XP[rows, lanes(j)].astype(F32)
            for half in range(2):
                D[perm(m, half, j), :] = delta[8 * half : 8 * half + 8]
                DX[perm(m, half, j), :] = dx[8 * half : 8 * half + 8]
        return carry

    lax.fori_loop(0, 16, prologue, 0)

    BP[...] = jnp.zeros((128, T), F32)
    BP[0:NS] = b_ref[...]
    BP[NS : 2 * NS] = c_ref[...]
    for tb in range(2):
        BTN[128 * tb : 128 * tb + 128, :] = BP[:, 128 * tb : 128 * tb + 128].T
    for i in range(STEPS):
        BTP[8 * i : 8 * i + 8, :] = BTN[pl.ds(i, 8, stride=STEPS), :]
    bt = BTP[...]
    hi = bt.astype(BF16)
    lo = (bt - hi.astype(F32)).astype(BF16)
    bt2 = jnp.concatenate([hi, lo], axis=1)

    def spread(g, carry):
        row = lax.broadcasted_iota(jnp.int32, (256, 512), 0) % 128
        col = lax.broadcasted_iota(jnp.int32, (256, 512), 1) // 128
        pick = jnp.where(row == col + 4 * g, 1.0, 0.0).astype(BF16)
        BB[g] = jnp.dot(bt2, pick, preferred_element_type=F32)
        return carry

    lax.fori_loop(0, 8, spread, 0)

    run = lax.broadcasted_iota(jnp.int32, (8, 128), 0)
    ones8 = jnp.ones((8, 128), F32)

    def roll(v, k):
        return pltpu.roll(v, k, axis=0)

    for j in range(3):
        total = D[j * T : j * T + 8, :]
        for i in range(1, STEPS):
            total = total + D[j * T + 8 * i : j * T + 8 * i + 8, :]
        upto = total
        for k in (1, 2, 4):
            upto = upto + jnp.where(run >= k, roll(upto, k), 0.0)
        CS[0, j] = total
        CS[1, j] = jnp.where(run >= 1, roll(upto, 1), 0.0)
        whole = jnp.broadcast_to(upto[7:8], (8, 128))
        CS[2, j] = whole - upto
        XF[s, j, NS : NS + 8, :] = whole

    def tiles(ref, ng):
        return [ref[ng, 8 * tt : 8 * tt + 8, :] for tt in range(12)]

    def at_step(ref, i):
        return [ref[pl.ds(pl.multiple_of(j * T + 8 * i, 8), 8), :] for j in range(3)]

    def of_states(g, i):
        return [BB[g, pl.ds(pl.multiple_of(8 * i, 8), 8), 128 * nn : 128 * nn + 128] for nn in range(4)]

    def local_forward(ng, carry):
        rates = tiles(A2B, ng)

        def step(i, hs):
            d, dx, b = at_step(D, i), at_step(DX, i), of_states(ng, i)
            new = []
            for tt in range(12):
                nn, j = tt // 3, tt % 3
                dec = jnp.exp2(d[j] * rates[tt])
                DEC[ng, i, 8 * tt : 8 * tt + 8, :] = dec
                new.append(dec * hs[tt] + b[nn] * dx[j])
            return tuple(new)

        ends = lax.fori_loop(0, STEPS, step, (jnp.zeros((8, 128), F32),) * 12, unroll=UNROLL)
        for tt in range(12):
            nn, j = tt // 3, tt % 3
            e, p = ends[tt], jnp.exp2(rates[tt] * CS[0, j])
            for k in (1, 2, 4):
                e = e + jnp.where(run >= k, p * roll(e, k), 0.0)
                p = jnp.where(run >= k, p * roll(p, k), p)
            HPRE[ng, 8 * tt : 8 * tt + 8, :] = jnp.where(run >= 1, roll(e, 1), 0.0)
            XF[s, j, pl.ds(4 * ng + nn, 1), :] = e[7:8]
        return carry

    lax.fori_loop(0, 4, local_forward, 0)

    f_copies = [rc(XF.at[s], XF.at[s], f_send.at[o], f_recv.at[o], (s + o) % 8, c) for o in range(1, 8)]
    for copy in f_copies:
        copy.start()
    for copy in f_copies:
        copy.wait_recv()

    def fold(table, reverse):
        for j in range(3):
            state = jnp.zeros((NS, 128), F32)
            for q in reversed(range(8)) if reverse else range(8):
                here = jnp.full((NS, 128), s, jnp.int32)
                valid = here < q if reverse else here > q
                dec = jnp.exp2(A2N[j] * XF[q, j, NS : NS + 1, :])
                state = jnp.where(valid, dec * state + table[q, j, :NS, :], state)
            HIN[j] = state

    fold(XF, False)

    def forward(ng, carry):
        rates = tiles(A2B, ng)
        hs = []
        for tt in range(12):
            nn, j = tt // 3, tt % 3
            begin = jnp.broadcast_to(HIN[j, pl.ds(4 * ng + nn, 1), :], (8, 128))
            h = HPRE[ng, 8 * tt : 8 * tt + 8, :] + jnp.exp2(rates[tt] * CS[1, j]) * begin
            HS[ng, 0, 8 * tt : 8 * tt + 8, :] = h
            hs.append(h)

        def step(i, hs):
            dx, b, cc = at_step(DX, i), of_states(ng, i), of_states(ng + 4, i)
            new, ys = [], [None] * 3
            for tt in range(12):
                nn, j = tt // 3, tt % 3
                dec = DEC[ng, i, 8 * tt : 8 * tt + 8, :]
                h = dec * hs[tt] + b[nn] * dx[j]
                HS[ng, i + 1, 8 * tt : 8 * tt + 8, :] = h
                ys[j] = cc[nn] * h if nn == 0 else ys[j] + cc[nn] * h
                new.append(h)
            for j in range(3):
                row = pl.ds(pl.multiple_of(j * T + 8 * i, 8), 8)
                Y[row, :] = Y[row, :] + ys[j]
            return tuple(new)

        lax.fori_loop(0, STEPS, step, tuple(hs), unroll=UNROLL)
        return carry

    Y[...] = jnp.zeros_like(Y)
    lax.fori_loop(0, 4, forward, 0)

    def natural(ref, m, j):
        return jnp.concatenate([ref[perm(m, 0, j), :], ref[perm(m, 1, j), :]], axis=0)

    def gate(m, carry):
        rows = pl.ds(pl.multiple_of(16 * m, 16), 16)
        for j in range(3):
            y = natural(Y, m, j) + SKP[0:1, lanes(j)] * XP[rows, lanes(j)].astype(F32)
            z = ZP[rows, lanes(j)].astype(F32)
            YN[rows, lanes(j)] = y
            GF[rows, lanes(j)] = y * z * sigmoid(z)
        return carry

    lax.fori_loop(0, 16, gate, 0)
    for j in range(3):
        for tb in range(2):
            cut = slice(128 * tb, 128 * tb + 128)
            GT[lanes(j), cut] = GF[cut, lanes(j)].T.astype(BF16)
    gt_copy = rc(GT.at[pl.ds(0, E)], GTP, p_send.at[4], p_recv.at[4], partner, c)
    gt_copy.start()

    w_copy.wait()
    for copy in gathers:
        copy.wait_recv()
    swaps = []
    for q in range(4):
        theirs = pl.ds(pl.multiple_of((2 * q + 1 - kap) * 2 * FEAT, 64), 2 * FEAT)
        swaps.append(rc(G.at[theirs], GP.at[q], p_send.at[q], p_recv.at[q], partner, c))
    for copy in swaps:
        copy.start()
    DGT[E:, :] = jnp.zeros((PAD - E, T), F32)
    DGT[:E, :] = jnp.dot(W[...], G[...], preferred_element_type=F32)
    for j in range(3):
        for tb in range(2):
            cut = slice(128 * tb, 128 * tb + 128)
            DG[cut, lanes(j)] = DGT[lanes(j), cut].T

    def ungate(m, sums):
        rows = pl.ds(pl.multiple_of(16 * m, 16), 16)
        new = []
        for j in range(3):
            z, dg = ZP[rows, lanes(j)].astype(F32), DG[rows, lanes(j)]
            sig = sigmoid(z)
            dy = dg * z * sig
            out = (dg * YN[rows, lanes(j)] * sig * (1.0 + z * (1.0 - sig))).astype(BF16)
            if j < 2:
                gg_ref[rows, lanes(j)] = out
            else:
                gg_ref[rows, 256:E] = out[:, : E - 256]
            for half in range(2):
                DY[perm(m, half, j), :] = dy[8 * half : 8 * half + 8]
            prod = dy * XP[rows, lanes(j)].astype(F32)
            new.append(sums[j] + prod[:8] + prod[8:])
        return tuple(new)

    skips = lax.fori_loop(0, 16, ungate, (jnp.zeros((8, 128), F32),) * 3)
    for j in range(3):
        XR[s, j, NS : NS + 8, :] = jnp.broadcast_to(jnp.sum(skips[j], axis=0, keepdims=True), (8, 128))

    def local_adjoint(ng, carry):
        def step(k, oms):
            i = STEPS - 1 - k
            dy, cc = at_step(DY, i), of_states(ng + 4, i)
            new, read = [], [None] * 4
            for tt in range(12):
                nn, j = tt // 3, tt % 3
                lam = cc[nn] * dy[j] + oms[tt]
                new.append(DEC[ng, i, 8 * tt : 8 * tt + 8, :] * lam)
                term = dy[j] * HS[ng, i + 1, 8 * tt : 8 * tt + 8, :]
                read[nn] = term if j == 0 else read[nn] + term
            for nn in range(4):
                PW[1, i, pl.ds(pl.multiple_of(32 * ng, 8) + 8 * nn, 8), :] = read[nn]
            return tuple(new)

        outs = lax.fori_loop(0, STEPS, step, (jnp.zeros((8, 128), F32),) * 12, unroll=UNROLL)
        rates = tiles(A2B, ng)
        for tt in range(12):
            nn, j = tt // 3, tt % 3
            e, p = outs[tt], jnp.exp2(rates[tt] * CS[0, j])
            for k in (1, 2, 4):
                e = e + jnp.where(run < 8 - k, p * roll(e, 8 - k), 0.0)
                p = jnp.where(run < 8 - k, p * roll(p, 8 - k), p)
            HPRE[ng, 8 * tt : 8 * tt + 8, :] = jnp.where(run < 7, roll(e, 7), 0.0)
            XB[s, j, pl.ds(4 * ng + nn, 1), :] = e[0:1]
        return carry

    lax.fori_loop(0, 4, local_adjoint, 0)
    b_copies = [rc(XB.at[s], XB.at[s], b_send.at[o], b_recv.at[o], (s + o) % 8, c) for o in range(1, 8)]
    for copy in b_copies:
        copy.start()

    gt_copy.wait_recv()
    for copy in swaps:
        copy.wait_recv()

    def weight_block(o):
        dest = (chip + o) % 4
        mine = G[pl.ds(pl.multiple_of((2 * dest + kap) * 2 * FEAT, 64), 2 * FEAT), :]
        dims = (((1,), (1,)), ((), ()))
        return lax.dot_general(GT[:E, :], mine, dims, preferred_element_type=F32) + lax.dot_general(
            GTP[...], GP[dest], dims, preferred_element_type=F32
        )

    half = E // 2
    SB[2, :, :E] = weight_block(2).astype(BF16)
    n_copies = [
        rc(SB.at[2, pl.ds(0, half)], RB.at[0], n_send.at[0], n_recv.at[0], up, c),
        rc(SB.at[2, pl.ds(half, half)], RB.at[1], n_send.at[1], n_recv.at[1], down, c),
    ]
    for copy in n_copies:
        copy.start()
    PB[0] = weight_block(1)
    PB[1] = weight_block(3)
    SB[0, half:, :E] = PB[0, half:, :].astype(BF16)
    SB[1, :half, :E] = PB[1, :half, :].astype(BF16)
    PB[2] = weight_block(0)
    late = [
        rc(SB.at[0, pl.ds(half, half)], RB.at[3], n_send.at[2], n_recv.at[2], up, c),
        rc(SB.at[1, pl.ds(0, half)], RB.at[4], n_send.at[3], n_recv.at[3], down, c),
    ]
    for copy in late:
        copy.start()

    for copy in b_copies:
        copy.wait_recv()
    fold(XB, True)

    for copy in n_copies:
        copy.wait_recv()
    SB[0, :half, :E] = (PB[0, :half, :] + RB[0, :, :E].astype(F32)).astype(BF16)
    SB[1, half:, :E] = (PB[1, half:, :] + RB[1, :, :E].astype(F32)).astype(BF16)

    def adjoint(ng, carry):
        rates = tiles(A2B, ng)
        oms = []
        for tt in range(12):
            nn, j = tt // 3, tt % 3
            begin = jnp.broadcast_to(HIN[j, pl.ds(4 * ng + nn, 1), :], (8, 128))
            oms.append(HPRE[ng, 8 * tt : 8 * tt + 8, :] + jnp.exp2(rates[tt] * CS[2, j]) * begin)

        def step(k, state):
            i = STEPS - 1 - k
            oms, accs = state
            d, dx, dy = at_step(D, i), at_step(DX, i), at_step(DY, i)
            b, cc = of_states(ng, i), of_states(ng + 4, i)
            new, acc = [], []
            lb, gd, write = [None] * 3, [None] * 3, [None] * 4
            for tt in range(12):
                nn, j = tt // 3, tt % 3
                lam = cc[nn] * dy[j] + oms[tt]
                om = DEC[ng, i, 8 * tt : 8 * tt + 8, :] * lam
                w = om * HS[ng, i, 8 * tt : 8 * tt + 8, :]
                new.append(om)
                acc.append(accs[tt] + w * d[j])
                lb[j] = lam * b[nn] if nn == 0 else lb[j] + lam * b[nn]
                gd[j] = w * rates[tt] if nn == 0 else gd[j] + w * rates[tt]
                write[nn] = lam * dx[j] if j == 0 else write[nn] + lam * dx[j]
            for nn in range(4):
                PW[0, i, pl.ds(pl.multiple_of(32 * ng, 8) + 8 * nn, 8), :] = write[nn]
            for j in range(3):
                row = pl.ds(pl.multiple_of(j * T + 8 * i, 8), 8)
                LB[row, :] = LB[row, :] + lb[j]
                GD[row, :] = GD[row, :] + gd[j]
            return tuple(new), tuple(acc)

        zeros = (jnp.zeros((8, 128), F32),) * 12
        _, accs = lax.fori_loop(0, STEPS, step, (tuple(oms), zeros), unroll=UNROLL)
        for tt in range(12):
            nn, j = tt // 3, tt % 3
            total = jnp.sum(accs[tt], axis=0, keepdims=True)
            XR[s, j, pl.ds(4 * ng + nn, 1), :] = LN2 * total * rates[tt][0:1]
        return carry

    LB[...] = jnp.zeros_like(LB)
    GD[...] = jnp.zeros_like(GD)
    final = [
        rc(SB.at[0, pl.ds(0, half)], RB.at[2], n_send.at[4], n_recv.at[4], up, c),
        rc(SB.at[1, pl.ds(half, half)], RB.at[5], n_send.at[5], n_recv.at[5], down, c),
    ]
    for copy in final:
        copy.start()
    lax.fori_loop(0, 4, adjoint, 0)
    r_copies = [rc(XR.at[s], XR.at[s], r_send.at[o], r_recv.at[o], (s + o) % 8, c) for o in range(1, 8)]
    for copy in r_copies:
        copy.start()

    def lane_sums(i, acc):
        col = lax.broadcasted_iota(jnp.int32, (256, 128), 1)
        row = lax.broadcasted_iota(jnp.int32, (256, 128), 0) // 128
        pick = jnp.where(col == i + 32 * row, 1.0, 0.0).astype(BF16)
        both = jnp.concatenate([PW[0, i], PW[1, i]], axis=1).astype(BF16)
        return acc + jnp.dot(both, pick, preferred_element_type=F32)

    sums = lax.fori_loop(0, STEPS, lane_sums, jnp.zeros((128, 128), F32), unroll=4)
    for n in range(NS):
        R2[pl.ds(n, 8, stride=NS), :] = sums[8 * n : 8 * n + 8]

    def x_rows(dest):
        return pl.ds(pl.multiple_of((dest // 2) * NS, NS), NS)

    x_copies = [
        rc(R2.at[x_rows((c + o) % 16)], GX.at[o], x_send.at[o], x_recv.at[o], s, (c + o) % 16)
        for o in range(1, 16)
    ]
    for copy in x_copies:
        copy.start()

    def epilogue(m, carry):
        rows = pl.ds(pl.multiple_of(16 * m, 16), 16)
        for j in range(3):
            x, st = XP[rows, lanes(j)].astype(F32), TP[rows, lanes(j)].astype(F32)
            lb = natural(LB, m, j)
            gi = (natural(D, m, j) * lb + natural(DY, m, j) * SKP[0:1, lanes(j)]).astype(BF16)
            gs = ((x * lb + LN2 * natural(GD, m, j)) * sigmoid(st)).astype(BF16)
            if j < 2:
                gi_ref[rows, lanes(j)] = gi
                gs_ref[rows, lanes(j)] = gs
            else:
                gi_ref[rows, 256:E] = gi[:, : E - 256]
                gs_ref[rows, 256:E] = gs[:, : E - 256]
        return carry

    lax.fori_loop(0, 16, epilogue, 0)

    for copy in r_copies:
        copy.wait_recv()
    for j in range(3):
        total = XR[0, j]
        for q in range(1, 8):
            total = total + XR[q, j]
        wide = 128 if j < 2 else E - 256
        gr_ref[:, 128 * j : 128 * j + wide] = total[:NS, :wide]
        gk_ref[:, 128 * j : 128 * j + wide] = total[NS : NS + 1, :wide]

    for copy in late + final:
        copy.wait_recv()
    gw_ref[:half, :] = PB[2, :half, :] + RB[2, :, :E].astype(F32) + RB[4, :, :E].astype(F32)
    gw_ref[half:, :] = PB[2, half:, :] + RB[3, :, :E].astype(F32) + RB[5, :, :E].astype(F32)

    for copy in x_copies:
        copy.wait_recv()
    mine = R2[x_rows(c), :]
    for o in range(1, 16):
        mine = mine + GX[o]
    odd = jnp.full((NS, NS), c % 2, jnp.int32) == 1
    gwrite_ref[...] = jnp.where(odd, mine[:, 16:32], mine[:, 0:16])
    gread_ref[...] = jnp.where(odd, mine[:, 48:64], mine[:, 32:48])

    for copy in gathers + f_copies + swaps + [gt_copy] + b_copies + n_copies + late + final + r_copies + x_copies:
        copy.wait_send()


SCRATCH = dict(
    W=((E, DM), BF16), G=((DM, T), BF16), GP=((4, 2 * FEAT, T), BF16), DOP=((T, 256), BF16),
    XP=((T, PAD), BF16), ZP=((T, PAD), BF16), TP=((T, PAD), BF16), SKP=((8, PAD), F32), LRP=((NS, PAD), F32),
    A2N=((3, NS, 128), F32), A2B=((4, 96, 128), F32), BP=((128, T), F32), BTN=((T, 128), F32), BTP=((T, 128), F32),
    BB=((8, T, 512), F32), D=((3 * T, 128), F32), DX=((3 * T, 128), F32), DY=((3 * T, 128), F32),
    Y=((3 * T, 128), F32), LB=((3 * T, 128), F32), GD=((3 * T, 128), F32),
    DEC=((4, STEPS, 96, 128), F32), HS=((4, STEPS + 1, 96, 128), F32), HPRE=((4, 96, 128), F32),
    HIN=((3, NS, 128), F32), PW=((2, STEPS, 128, 128), F32), CS=((3, 3, 8, 128), F32),
    YN=((T, PAD), F32), GF=((T, PAD), F32), GT=((PAD, T), BF16), GTP=((E, T), BF16),
    DGT=((PAD, T), F32), DG=((T, PAD), F32), PB=((3, E, E), F32), SB=((3, E, PAD), BF16), RB=((6, E // 2, PAD), BF16),
    XF=((8, 3, 24, 128), F32), XB=((8, 3, NS, 128), F32), XR=((8, 3, 24, 128), F32),
    R2=((128, 128), F32), GX=((16, NS, 128), F32),
)
SEMS = (None, 16, 16, 5, 5, 8, 8, 8, 8, 8, 8, 6, 6, 16, 16)


def on_device(x, z, st, lr, sk, b, c, w, do):
    vmem, shape = pl.BlockSpec(memory_space=pltpu.VMEM), jax.ShapeDtypeStruct
    dma = pltpu.SemaphoreType.DMA
    outs = pl.pallas_call(
        kernel,
        out_shape=(
            shape((T, E), BF16), shape((T, E), BF16), shape((T, E), BF16), shape((NS, E), F32), shape((1, E), F32),
            shape((NS, NS), F32), shape((NS, NS), F32), shape((E, E), F32),
        ),
        in_specs=[vmem] * 7 + [pl.BlockSpec(memory_space=pl.ANY), vmem],
        out_specs=(vmem,) * 8,
        scratch_shapes=[pltpu.VMEM(*v) for v in SCRATCH.values()] + [dma if n is None else dma((n,)) for n in SEMS],
        compiler_params=pltpu.CompilerParams(
            collective_id=0, has_side_effects=True, vmem_limit_bytes=60 * 1024 * 1024
        ),
    )(x, z, st, lr, sk.reshape(1, E), b, c, w, do)
    return outs[:4] + (outs[4].reshape(E),) + outs[5:]


def solution(mesh):
    return jax.shard_map(
        on_device,
        mesh=mesh,
        in_specs=(
            P("seq", "chan"), P("seq", "chan"), P("seq", "chan"), P(None, "chan"), P("chan"),
            P(None, "seq"), P(None, "seq"), P("chan", None), P("seq", "chan"),
        ),
        out_specs=(
            P("seq", "chan"), P("seq", "chan"), P("seq", "chan"), P(None, "chan"), P("chan"),
            P(None, ("seq", "chan")), P(None, ("seq", "chan")), P("chan", "seq"),
        ),
        check_vma=False,
    )
```

profile of v0, /device:TPU:0, one launch (start us, length us, event | category | flops | bytes accessed | tf_op | source)
XLA Modules:
  0.0 72.3 jit_solution(17072960933862504299)
XLA Ops:
  0.6 1.2 %reshape.22.sk_ref = f32[1,320]{1,0:T(1,128)} reshape(f32[320]{0:T(512)} %param.13) | data formatting | bytes 2560 | tf_op jit(solution)/shard_map/reshape | solution.py:508
  1.9 1.6 %copy.20.do_ref = bf16[256,160]{1,0:T(8,128)(2,1)} copy(bf16[256,160]{0,1:T(8,128)(2,1)} %param.17) | data formatting | bytes 163840 | tf_op args[8]
  3.5 1.7 %copy.17.x_ref = bf16[256,320]{1,0:T(8,128)(2,1)} copy(bf16[256,320]{0,1:T(8,128)(2,1)} %param.9) | data formatting | bytes 327680 | tf_op args[0]
  5.3 1.7 %copy.18.z_ref = bf16[256,320]{1,0:T(8,128)(2,1)} copy(bf16[256,320]{0,1:T(8,128)(2,1)} %param.10) | data formatting | bytes 327680 | tf_op args[1]
  7.0 1.7 %copy.19.st_ref = bf16[256,320]{1,0:T(8,128)(2,1)} copy(bf16[256,320]{0,1:T(8,128)(2,1)} %param.11) | data formatting | bytes 327680 | tf_op args[2]
  8.7 51.5 %shard_map.152 = (bf16[256,320]{1,0:T(8,128)(2,1)}, bf16[256,320]{1,0:T(8,128)(2,1)}, bf16[256,320]{1,0:T(8,128)(2,1)}, f32[16,320]{1,0:T(8,128)}, f32[1,320]{1,...) custom-call(bf16[256,320]{1,0:T(8,128)(2,1)} %copy.17.x_ref, bf16[256,320]{1,0:T(8,128)(2,1)} %copy.18.z_ref, ...), custom_call_target="tpu_custom_call" | custom-call | tf_op jit(solution)/shard_map/pallas_call | solution.py:496
  60.2 1.7 %copy.21 = bf16[256,320]{0,1:T(8,128)(2,1)} copy(bf16[256,320]{1,0:T(8,128)(2,1)} %get-tuple-element.24) | data formatting | bytes 327680
  61.9 1.2 %reduce = f32[320]{0:T(512)} reduce(f32[1,320]{1,0:T(1,128)} %get-tuple-element.20, f32[]{:T(128)} %constant), dimensions={0}, to_apply=%get-tuple-element.20.reduce_sub_computation | reduce | bytes 2564 | tf_op jit(solution)/shard_map/pallas_call | solution.py:496
  63.1 1.7 %copy.22 = bf16[256,320]{0,1:T(8,128)(2,1)} copy(bf16[256,320]{1,0:T(8,128)(2,1)} %get-tuple-element.25) | data formatting | bytes 327680
  64.8 1.7 %copy.23 = bf16[256,320]{0,1:T(8,128)(2,1)} copy(bf16[256,320]{1,0:T(8,128)(2,1)} %get-tuple-element.26) | data formatting | bytes 327680
  66.5 1.3 %copy.28 = f32[16,320]{1,0:T(8,128)} copy(f32[16,320]{1,0:T(8,128)} %get-tuple-element.43) | data formatting | bytes 40960
  67.9 1.3 %copy.29 = f32[16,16]{1,0:T(8,128)} copy(f32[16,16]{1,0:T(8,128)} %get-tuple-element.45) | data formatting | bytes 2048
  69.2 1.3 %copy.30 = f32[16,16]{1,0:T(8,128)} copy(f32[16,16]{1,0:T(8,128)} %get-tuple-element.46) | data formatting | bytes 2048
  70.5 1.8 %copy.31 = f32[320,320]{1,0:T(8,128)} copy(f32[320,320]{1,0:T(8,128)} %get-tuple-element.47) | data formatting | bytes 819200
where the time goes:
time: 72.8 us; the launch traced here: 72.3 us
  Pallas kernels  51.5 us (71%)
  local copies, waits for them, and re-layouts  19 us (26%)
  other arithmetic  1.2 us (2%)
    pallas_call x1, Pallas kernels, on_device(): pl.pallas_call(kernel, out_shape=(shape((T, E), BF16), shape((T, E), BF16...  51.5 us
    unnamed x11, local copies, waits for them, and re-layouts  17.7 us

commit v1 on v0

--- a/solution.py
+++ b/solution.py
@@ -1,4 +1,3 @@
-import functools
 import math
 
 import jax
@@ -20,14 +19,29 @@
     return 1.0 / (1.0 + jnp.exp(-v))
 
 
+class Phases:
+    def __init__(self):
+        self.now = None
+
+    def __call__(self, name):
+        if self.now is not None:
+            self.now.__exit__(None, None, None)
+        self.now = jax.named_scope(name) if name else None
+        if self.now is not None:
+            self.now.__enter__()
+
+
 def kernel(
     x_ref, z_ref, st_ref, lr_ref, sk_ref, b_ref, c_ref, w_hbm, do_ref,
+    gi_hbm, gg_hbm, gs_hbm, gr_hbm, gk_hbm, gwrite_hbm, gread_hbm, gw_hbm,
     gi_ref, gg_ref, gs_ref, gr_ref, gk_ref, gwrite_ref, gread_ref, gw_ref,
-    W, G, GP, DOP, XP, ZP, TP, SKP, LRP, A2N, A2B, BP, BTN, BTP, BB, D, DX, DY, Y, LB, GD,
-    DEC, HS, HPRE, HIN, PW, CS, YN, GF, GT, GTP, DGT, DG, PB, SB, RB, XF, XB, XR, R2, GX,
-    w_sem, g_send, g_recv, p_send, p_recv, f_send, f_recv, b_send, b_recv, r_send, r_recv,
+    W, G, GP, SKB, LRP, A2N, A2B, BP, BTN, BTP, BB, DT, DXT, D, DX, DY, Y, LB, GD,
+    DEC, HS, HPRE, HIN, PW, CS, YT, GDT, SILU, GT, GTP, PB, SB, RB, XF, XB, XR, R2, GX,
+    w_sem, o_sem, g_send, g_recv, p_send, p_recv, f_send, f_recv, b_send, b_recv, r_send, r_recv,
     n_send, n_recv, x_send, x_recv,
 ):
+    phase = Phases()
+    phase("enter")
     s, c = lax.axis_index("seq"), lax.axis_index("chan")
     kap, chip = s % 2, s // 2
     partner = s + 1 - 2 * kap
@@ -47,30 +61,19 @@
     for o in range(1, 8):
         pl.semaphore_signal(barrier, inc=1, device_id=((s + o) % 8, c), device_id_type=pl.DeviceIdType.MESH)
 
-    DOP[:, FEAT:] = jnp.zeros((T, 256 - FEAT), BF16)
-    DOP[:, :FEAT] = do_ref[...]
     own = pl.multiple_of(c * FEAT, 32)
-    for tb in range(2):
-        rows = slice(128 * tb, 128 * tb + 128)
-        first = DOP[rows, :128].astype(F32).T.astype(BF16)
-        second = DOP[rows, 128:].astype(F32).T.astype(BF16)
-        G[pl.ds(own, 128), rows] = first
-        G[pl.ds(own + 128, FEAT - 128), rows] = second[: FEAT - 128]
+    G[pl.ds(own, FEAT), :] = do_ref[...]
     pl.semaphore_wait(barrier, 22)
 
     def g_copy(o):
         q = pl.ds(own, FEAT)
-        return rc(G.at[q], G.at[q], g_send.at[o], g_recv.at[o], s, (c + o) % 16)
+        return rc(do_ref, G.at[q], g_send.at[o], g_recv.at[o], s, (c + o) % 16)
 
     gathers = [g_copy(o) for o in range(1, 16)]
     for copy in gathers:
         copy.start()
 
-    for src, dst in ((x_ref, XP), (z_ref, ZP), (st_ref, TP)):
-        dst[:, 256:] = jnp.zeros((T, 128), BF16)
-        dst[:, :E] = src[...]
-    SKP[:, 256:] = jnp.zeros((8, 128), F32)
-    SKP[0:1, :E] = sk_ref[...]
+    phase("prologue")
     LRP[:, 256:] = jnp.zeros((NS, 128), F32)
     LRP[:, :E] = lr_ref[...]
     for j in range(3):
@@ -79,26 +82,48 @@
         for j in range(3):
             tt = (n % 4) * 3 + j
             A2B[n // 4, 8 * tt : 8 * tt + 8, :] = jnp.broadcast_to(A2N[j, n : n + 1, :], (8, 128))
+    LRP[0:1, :E] = sk_ref[...].reshape(1, E)
+    for j in range(3):
+        SKB[128 * j : 128 * j + 128, :] = jnp.broadcast_to(LRP[0:1, 128 * j : 128 * j + 128], (128, 128)).T
 
     def lanes(j):
         return slice(128 * j, 128 * j + 128)
 
-    def perm(m, half, j):
-        return pl.ds(j * T + 8 * (16 * (m % 2) + 8 * half) + m // 2, 8, stride=8)
+    def block(m):
+        return pl.ds(pl.multiple_of(16 * m, 16), 16)
 
     def prologue(m, carry):
-        rows = pl.ds(pl.multiple_of(16 * m, 16), 16)
+        rows = block(m)
+        st = st_ref[rows, :].astype(F32)
+        delta = jnp.maximum(st, 0.0) + jnp.log1p(jnp.exp(-jnp.abs(st)))
+        DT[rows, :] = delta
+        DXT[rows, :] = delta * x_ref[rows, :].astype(F32)
+        return carry
+
+    DT[E:, :] = jnp.zeros((PAD - E, T), F32)
+    DXT[E:, :] = jnp.zeros((PAD - E, T), F32)
+    lax.fori_loop(0, E // 16, prologue, 0, unroll=2)
+
+    def places():
         for j in range(3):
-            st = TP[rows, lanes(j)].astype(F32)
-            delta = jnp.maximum(st, 0.0) + jnp.log1p(jnp.exp(-jnp.abs(st)))
-            dx = delta * XP[rows, lanes(j)].astype(F32)
-            for half in range(2):
-                D[perm(m, half, j), :] = delta[8 * half : 8 * half + 8]
-                DX[perm(m, half, j), :] = dx[8 * half : 8 * half + 8]
-        return carry
-
-    lax.fori_loop(0, 16, prologue, 0)
-
+            for tb in range(2):
+                at = [pl.ds(j * T + 8 * (8 * (q % 4)) + 4 * tb + q // 4, 8, stride=8) for q in range(16)]
+                yield lanes(j), lanes(tb), at
+
+    def by_step(src, dst):
+        for rows, cols, at in places():
+            turned = src[rows, cols].T
+            for q in range(16):
+                dst[at[q], :] = turned[8 * q : 8 * q + 8]
+
+    def by_channel(src, dst):
+        for rows, cols, at in places():
+            dst[rows, cols] = jnp.concatenate([src[at[q], :] for q in range(16)], axis=0).T
+
+    by_step(DT, D)
+    by_step(DXT, DX)
+
+    phase("spread")
     BP[...] = jnp.zeros((128, T), F32)
     BP[0:NS] = b_ref[...]
     BP[NS : 2 * NS] = c_ref[...]
@@ -148,6 +173,7 @@
     def of_states(g, i):
         return [BB[g, pl.ds(pl.multiple_of(8 * i, 8), 8), 128 * nn : 128 * nn + 128] for nn in range(4)]
 
+    phase("pass1")
     def local_forward(ng, carry):
         rates = tiles(A2B, ng)
 
@@ -174,6 +200,7 @@
 
     lax.fori_loop(0, 4, local_forward, 0)
 
+    phase("fexchange")
     f_copies = [rc(XF.at[s], XF.at[s], f_send.at[o], f_recv.at[o], (s + o) % 8, c) for o in range(1, 8)]
     for copy in f_copies:
         copy.start()
@@ -192,6 +219,7 @@
 
     fold(XF, False)
 
+    phase("pass2")
     def forward(ng, carry):
         rates = tiles(A2B, ng)
         hs = []
@@ -223,26 +251,25 @@
     Y[...] = jnp.zeros_like(Y)
     lax.fori_loop(0, 4, forward, 0)
 
-    def natural(ref, m, j):
-        return jnp.concatenate([ref[perm(m, 0, j), :], ref[perm(m, 1, j), :]], axis=0)
+    phase("gate")
+    by_channel(Y, YT)
 
     def gate(m, carry):
-        rows = pl.ds(pl.multiple_of(16 * m, 16), 16)
-        for j in range(3):
-            y = natural(Y, m, j) + SKP[0:1, lanes(j)] * XP[rows, lanes(j)].astype(F32)
-            z = ZP[rows, lanes(j)].astype(F32)
-            YN[rows, lanes(j)] = y
-            GF[rows, lanes(j)] = y * z * sigmoid(z)
-        return carry
-
-    lax.fori_loop(0, 16, gate, 0)
-    for j in range(3):
-        for tb in range(2):
-            cut = slice(128 * tb, 128 * tb + 128)
-            GT[lanes(j), cut] = GF[cut, lanes(j)].T.astype(BF16)
-    gt_copy = rc(GT.at[pl.ds(0, E)], GTP, p_send.at[4], p_recv.at[4], partner, c)
+        rows = block(m)
+        skip = SKB[rows, :]
+        y = YT[rows, :] + jnp.concatenate([skip, skip], axis=1) * x_ref[rows, :].astype(F32)
+        z = z_ref[rows, :].astype(F32)
+        sig = sigmoid(z)
+        SILU[rows, :] = z * sig
+        GT[rows, :] = (y * z * sig).astype(BF16)
+        YT[rows, :] = y * sig * (1.0 + z * (1.0 - sig))
+        return carry
+
+    lax.fori_loop(0, E // 16, gate, 0, unroll=2)
+    gt_copy = rc(GT, GTP, p_send.at[4], p_recv.at[4], partner, c)
     gt_copy.start()
 
+    phase("gwait")
     w_copy.wait()
     for copy in gathers:
         copy.wait_recv()
@@ -252,35 +279,26 @@
         swaps.append(rc(G.at[theirs], GP.at[q], p_send.at[q], p_recv.at[q], partner, c))
     for copy in swaps:
         copy.start()
-    DGT[E:, :] = jnp.zeros((PAD - E, T), F32)
-    DGT[:E, :] = jnp.dot(W[...], G[...], preferred_element_type=F32)
+    phase("dg")
     for j in range(3):
-        for tb in range(2):
-            cut = slice(128 * tb, 128 * tb + 128)
-            DG[cut, lanes(j)] = DGT[lanes(j), cut].T
-
-    def ungate(m, sums):
-        rows = pl.ds(pl.multiple_of(16 * m, 16), 16)
-        new = []
-        for j in range(3):
-            z, dg = ZP[rows, lanes(j)].astype(F32), DG[rows, lanes(j)]
-            sig = sigmoid(z)
-            dy = dg * z * sig
-            out = (dg * YN[rows, lanes(j)] * sig * (1.0 + z * (1.0 - sig))).astype(BF16)
-            if j < 2:
-                gg_ref[rows, lanes(j)] = out
-            else:
-                gg_ref[rows, 256:E] = out[:, : E - 256]
-            for half in range(2):
-                DY[perm(m, half, j), :] = dy[8 * half : 8 * half + 8]
-            prod = dy * XP[rows, lanes(j)].astype(F32)
-            new.append(sums[j] + prod[:8] + prod[8:])
-        return tuple(new)
-
-    skips = lax.fori_loop(0, 16, ungate, (jnp.zeros((8, 128), F32),) * 3)
+        rows = slice(128 * j, min(128 * j + 128, E))
+        dg = jnp.dot(W[rows, :], G[...], preferred_element_type=F32)
+        dy = dg * SILU[rows, :]
+        DXT[rows, :] = dy
+        gg_ref[rows, :] = (dg * YT[rows, :]).astype(BF16)
+        SILU[rows, :] = dy * x_ref[rows, :].astype(F32)
+    gg_out = pltpu.make_async_copy(gg_ref, gg_hbm, o_sem.at[1])
+    gg_out.start()
+    by_step(DXT, DY)
+    ones = jnp.ones((8, T), BF16)
+    skips = lax.dot_general(ones, SILU[...].astype(BF16), (((1,), (1,)), ((), ())), preferred_element_type=F32)
     for j in range(3):
-        XR[s, j, NS : NS + 8, :] = jnp.broadcast_to(jnp.sum(skips[j], axis=0, keepdims=True), (8, 128))
-
+        wide = 128 if j < 2 else E - 256
+        if j == 2:
+            XR[s, j, NS : NS + 8, :] = jnp.zeros((8, 128), F32)
+        XR[s, j, NS : NS + 8, :wide] = skips[:, 128 * j : 128 * j + wide]
+
+    phase("pass3")
     def local_adjoint(ng, carry):
         def step(k, oms):
             i = STEPS - 1 - k
@@ -309,6 +327,7 @@
         return carry
 
     lax.fori_loop(0, 4, local_adjoint, 0)
+    phase("weight")
     b_copies = [rc(XB.at[s], XB.at[s], b_send.at[o], b_recv.at[o], (s + o) % 8, c) for o in range(1, 8)]
     for copy in b_copies:
         copy.start()
@@ -321,7 +340,7 @@
         dest = (chip + o) % 4
         mine = G[pl.ds(pl.multiple_of((2 * dest + kap) * 2 * FEAT, 64), 2 * FEAT), :]
         dims = (((1,), (1,)), ((), ()))
-        return lax.dot_general(GT[:E, :], mine, dims, preferred_element_type=F32) + lax.dot_general(
+        return lax.dot_general(GT[...], mine, dims, preferred_element_type=F32) + lax.dot_general(
             GTP[...], GP[dest], dims, preferred_element_type=F32
         )
 
@@ -345,15 +364,18 @@
     for copy in late:
         copy.start()
 
+    phase("bwait")
     for copy in b_copies:
         copy.wait_recv()
     fold(XB, True)
 
+    phase("nwait")
     for copy in n_copies:
         copy.wait_recv()
     SB[0, :half, :E] = (PB[0, :half, :] + RB[0, :, :E].astype(F32)).astype(BF16)
     SB[1, half:, :E] = (PB[1, half:, :] + RB[1, :, :E].astype(F32)).astype(BF16)
 
+    phase("pass4")
     def adjoint(ng, carry):
         rates = tiles(A2B, ng)
         oms = []
@@ -404,6 +426,7 @@
     for copy in final:
         copy.start()
     lax.fori_loop(0, 4, adjoint, 0)
+    phase("lanesums")
     r_copies = [rc(XR.at[s], XR.at[s], r_send.at[o], r_recv.at[o], (s + o) % 8, c) for o in range(1, 8)]
     for copy in r_copies:
         copy.start()
@@ -429,23 +452,28 @@
     for copy in x_copies:
         copy.start()
 
+    phase("epilogue")
+    by_channel(LB, YT)
+    by_channel(GD, GDT)
+
     def epilogue(m, carry):
-        rows = pl.ds(pl.multiple_of(16 * m, 16), 16)
-        for j in range(3):
-            x, st = XP[rows, lanes(j)].astype(F32), TP[rows, lanes(j)].astype(F32)
-            lb = natural(LB, m, j)
-            gi = (natural(D, m, j) * lb + natural(DY, m, j) * SKP[0:1, lanes(j)]).astype(BF16)
-            gs = ((x * lb + LN2 * natural(GD, m, j)) * sigmoid(st)).astype(BF16)
-            if j < 2:
-                gi_ref[rows, lanes(j)] = gi
-                gs_ref[rows, lanes(j)] = gs
-            else:
-                gi_ref[rows, 256:E] = gi[:, : E - 256]
-                gs_ref[rows, 256:E] = gs[:, : E - 256]
-        return carry
-
-    lax.fori_loop(0, 16, epilogue, 0)
-
+        rows = block(m)
+        skip, lb = SKB[rows, :], YT[rows, :]
+        dy = DXT[rows, :]
+        gi_ref[rows, :] = (DT[rows, :] * lb + dy * jnp.concatenate([skip, skip], axis=1)).astype(BF16)
+        gd = x_ref[rows, :].astype(F32) * lb + LN2 * GDT[rows, :]
+        gs_ref[rows, :] = (gd * sigmoid(st_ref[rows, :].astype(F32))).astype(BF16)
+        return carry
+
+    lax.fori_loop(0, E // 16, epilogue, 0, unroll=2)
+    outs = [
+        pltpu.make_async_copy(gi_ref, gi_hbm, o_sem.at[0]),
+        pltpu.make_async_copy(gs_ref, gs_hbm, o_sem.at[2]),
+    ]
+    for copy in outs:
+        copy.start()
+
+    phase("rwait")
     for copy in r_copies:
         copy.wait_recv()
     for j in range(3):
@@ -455,12 +483,14 @@
         wide = 128 if j < 2 else E - 256
         gr_ref[:, 128 * j : 128 * j + wide] = total[:NS, :wide]
         gk_ref[:, 128 * j : 128 * j + wide] = total[NS : NS + 1, :wide]
+    phase("gw")
 
     for copy in late + final:
         copy.wait_recv()
     gw_ref[:half, :] = PB[2, :half, :] + RB[2, :, :E].astype(F32) + RB[4, :, :E].astype(F32)
     gw_ref[half:, :] = PB[2, half:, :] + RB[3, :, :E].astype(F32) + RB[5, :, :E].astype(F32)
 
+    phase("xwait")
     for copy in x_copies:
         copy.wait_recv()
     mine = R2[x_rows(c), :]
@@ -470,43 +500,81 @@
     gwrite_ref[...] = jnp.where(odd, mine[:, 16:32], mine[:, 0:16])
     gread_ref[...] = jnp.where(odd, mine[:, 48:64], mine[:, 32:48])
 
+    phase("leave")
+    pairs = ((gr_ref, gr_hbm), (gk_ref, gk_hbm), (gwrite_ref, gwrite_hbm), (gread_ref, gread_hbm), (gw_ref, gw_hbm))
+    for k, (src, dst) in enumerate(pairs):
+        outs.append(pltpu.make_async_copy(src, dst, o_sem.at[3 + k]))
+        outs[-1].start()
     for copy in gathers + f_copies + swaps + [gt_copy] + b_copies + n_copies + late + final + r_copies + x_copies:
         copy.wait_send()
-
-
+    for copy in outs + [gg_out]:
+        copy.wait()
+    phase(None)
+
+
+def finish(*refs):
+    srcs, dsts, bufs, sems = refs[:8], refs[8:16], refs[16:24], refs[24:]
+    ins = [pltpu.make_async_copy(a, v, sems[0].at[k]) for k, (a, v) in enumerate(zip(srcs, bufs))]
+    outs = [pltpu.make_async_copy(v, a, sems[1].at[k]) for k, (a, v) in enumerate(zip(dsts, bufs)) if k != 4]
+    for copy in ins:
+        copy.start()
+    for copy in ins:
+        copy.wait()
+    for copy in outs:
+        copy.start()
+    dsts[4][...] = bufs[4][...].reshape(E)
+    for copy in outs:
+        copy.wait()
+
+
+RESULTS = (
+    ((E, T), BF16), ((E, T), BF16), ((E, T), BF16), ((NS, E), F32), ((1, E), F32),
+    ((NS, NS), F32), ((NS, NS), F32), ((E, E), F32),
+)
 SCRATCH = dict(
-    W=((E, DM), BF16), G=((DM, T), BF16), GP=((4, 2 * FEAT, T), BF16), DOP=((T, 256), BF16),
-    XP=((T, PAD), BF16), ZP=((T, PAD), BF16), TP=((T, PAD), BF16), SKP=((8, PAD), F32), LRP=((NS, PAD), F32),
+    W=((E, DM), BF16), G=((DM, T), BF16), GP=((4, 2 * FEAT, T), BF16), SKB=((PAD, 128), F32), LRP=((NS, PAD), F32),
     A2N=((3, NS, 128), F32), A2B=((4, 96, 128), F32), BP=((128, T), F32), BTN=((T, 128), F32), BTP=((T, 128), F32),
-    BB=((8, T, 512), F32), D=((3 * T, 128), F32), DX=((3 * T, 128), F32), DY=((3 * T, 128), F32),
+    BB=((8, T, 512), F32), DT=((PAD, T), F32), DXT=((PAD, T), F32),
+    D=((3 * T, 128), F32), DX=((3 * T, 128), F32), DY=((3 * T, 128), F32),
     Y=((3 * T, 128), F32), LB=((3 * T, 128), F32), GD=((3 * T, 128), F32),
     DEC=((4, STEPS, 96, 128), F32), HS=((4, STEPS + 1, 96, 128), F32), HPRE=((4, 96, 128), F32),
     HIN=((3, NS, 128), F32), PW=((2, STEPS, 128, 128), F32), CS=((3, 3, 8, 128), F32),
-    YN=((T, PAD), F32), GF=((T, PAD), F32), GT=((PAD, T), BF16), GTP=((E, T), BF16),
-    DGT=((PAD, T), F32), DG=((T, PAD), F32), PB=((3, E, E), F32), SB=((3, E, PAD), BF16), RB=((6, E // 2, PAD), BF16),
+    YT=((PAD, T), F32), GDT=((PAD, T), F32), SILU=((E, T), F32), GT=((E, T), BF16), GTP=((E, T), BF16),
+    PB=((3, E, E), F32), SB=((3, E, PAD), BF16), RB=((6, E // 2, PAD), BF16),
     XF=((8, 3, 24, 128), F32), XB=((8, 3, NS, 128), F32), XR=((8, 3, 24, 128), F32),
     R2=((128, 128), F32), GX=((16, NS, 128), F32),
 )
-SEMS = (None, 16, 16, 5, 5, 8, 8, 8, 8, 8, 8, 6, 6, 16, 16)
+SEMS = (None, 8, 16, 16, 5, 5, 8, 8, 8, 8, 8, 8, 6, 6, 16, 16)
 
 
 def on_device(x, z, st, lr, sk, b, c, w, do):
-    vmem, shape = pl.BlockSpec(memory_space=pltpu.VMEM), jax.ShapeDtypeStruct
+    vmem, hbm = pl.BlockSpec(memory_space=pltpu.VMEM), pl.BlockSpec(memory_space=pl.ANY)
     dma = pltpu.SemaphoreType.DMA
-    outs = pl.pallas_call(
+    buffers = [pltpu.VMEM(*v) for v in RESULTS]
+    parts = pl.pallas_call(
         kernel,
-        out_shape=(
-            shape((T, E), BF16), shape((T, E), BF16), shape((T, E), BF16), shape((NS, E), F32), shape((1, E), F32),
-            shape((NS, NS), F32), shape((NS, NS), F32), shape((E, E), F32),
-        ),
-        in_specs=[vmem] * 7 + [pl.BlockSpec(memory_space=pl.ANY), vmem],
-        out_specs=(vmem,) * 8,
-        scratch_shapes=[pltpu.VMEM(*v) for v in SCRATCH.values()] + [dma if n is None else dma((n,)) for n in SEMS],
+        out_shape=[jax.ShapeDtypeStruct(*v) for v in RESULTS],
+        in_specs=[vmem] * 7 + [hbm, vmem],
+        out_specs=[hbm] * 8,
+        scratch_shapes=buffers
+        + [pltpu.VMEM(*v) for v in SCRATCH.values()]
+        + [dma if n is None else dma((n,)) for n in SEMS],
         compiler_params=pltpu.CompilerParams(
             collective_id=0, has_side_effects=True, vmem_limit_bytes=60 * 1024 * 1024
         ),
-    )(x, z, st, lr, sk.reshape(1, E), b, c, w, do)
-    return outs[:4] + (outs[4].reshape(E),) + outs[5:]
+    )(x.T, z.T, st.T, lr, sk, b, c, w, do.T)
+    shapes = [jax.ShapeDtypeStruct(*v) for v in RESULTS]
+    shapes[4] = jax.ShapeDtypeStruct((E,), F32)
+    specs = [hbm] * 8
+    specs[4] = vmem
+    outs = pl.pallas_call(
+        finish,
+        out_shape=shapes,
+        in_specs=[hbm] * 8,
+        out_specs=specs,
+        scratch_shapes=buffers + [dma((8,)), dma((8,))],
+    )(*parts)
+    return (outs[0].T, outs[1].T, outs[2].T, *outs[3:])
 
 
 def solution(mesh):

time: 72.8 us -> 54.7 us (0.75)
  local copies, waits for them, and re-layouts: 19 us -> 0 us
  Pallas kernels: 51.5 us -> 53.9 us
  other arithmetic: 1.2 us -> 0 us
    unnamed x11 -> x0, local copies, waits for them, and re-layouts: 17.7 us -> none
    pallas_call x1 -> x2, Pallas kernels: 51.5 us -> 53.9 us  [the longest x1 50.9 us: on_device(): pl.pallas_call(kernel, out_shape=[jax.ShapeDtypeStruct(*v) for v in RESUL...]
    reshape x1 -> x0, local copies, waits for them, and re-layouts: 1.25 us -> none  [on_device(): sk.reshape(1, E)]
    pallas_call x1 -> x0, other arithmetic: 1.2 us -> none  [on_device(): pl.pallas_call(kernel, out_shape=(shape((T, E), BF16), shape((T, E), BF16...]
where the time goes in v1:
time: 54.7 us; the launch traced here: 54.5 us
  Pallas kernels  53.9 us (99%)
  between operations  0.64 us (1%)
    pallas_call x1, Pallas kernels, on_device(): pl.pallas_call(kernel, out_shape=[jax.ShapeDtypeStruct(*v) for v in RESUL...  50.9 us
    pallas_call x1, Pallas kernels, on_device(): pl.pallas_call(finish, out_shape=shapes, in_specs=[hbm] * 8, out_specs=sp...  2.99 us

profile of v1, /device:TPU:0, one launch (start us, length us, event | category | flops | bytes accessed | tf_op | source)
XLA Modules:
  0.0 54.5 jit_solution(12343016267191603989)
XLA Ops:
  0.6 50.9 %shard_map.152 = (bf16[320,256]{1,0:T(8,128)(2,1)}, bf16[320,256]{1,0:T(8,128)(2,1)}, bf16[320,256]{1,0:T(8,128)(2,1)}, f32[16,320]{1,0:T(8,128)}, f32[1,320]{1,...) custom-call(bf16[320,256]{1,0:T(8,128)(2,1)} %bitcast.7, bf16[320,256]{1,0:T(8,128)(2,1)} %bitcast.8, ...), custom_call_target="tpu_custom_call" | custom-call | tf_op jit(solution)/shard_map/pallas_call | solution.py:554
  51.5 3.0 %shard_map.153 = (bf16[320,256]{1,0:T(8,128)(2,1)}, bf16[320,256]{1,0:T(8,128)(2,1)}, bf16[320,256]{1,0:T(8,128)(2,1)}, f32[16,320]{1,0:T(8,128)}, f32[320]{0:T(...) custom-call(bf16[320,256]{1,0:T(8,128)(2,1)} %get-tuple-element.24.refs_0_, ...), custom_call_target="tpu_custom_call" | custom-call | tf_op jit(solution)/shard_map/pallas_call | solution.py:570
